TPU v7x, 32 devices: a whole 2x2x4 slice. The times are simulated.
32 devices in a mesh: grp: 2 (over x), seq: 8 (over z, y), kv: 2 (over core).
Axes of the slice: x: 2, y: 2, z: 4, core: 2. Of those that a mesh axis runs over, the one named last changes fastest.
Arguments:
- queries: bfloat16 [4, 64, 128], P(('grp', 'kv'), 'seq'), parts along dimension 0, may hold values from -256 to 256
- keys: bfloat16 [4, 16384, 8, 128], P(('grp', 'kv'), 'seq'), parts along dimension 0, may hold values from -6 to 6
- values: bfloat16 [4, 16384, 8, 128], P(('grp', 'kv'), 'seq'), parts along dimension 0, may hold values from -6 to 6
- picks: int32 [4, 64, 3], P(('grp', 'kv'), 'seq'), parts along dimension 0, may hold values from 0 to 31, as said below
- lengths: int32 [4], P(('grp', 'kv')), parts along dimension 0, may hold values from 8194 to 16384, as said below
Outputs:
- attended: bfloat16 [4, 64, 128], P(('grp', 'kv'), 'seq'), parts along dimension 0
There are 2 independent parts, one for each index of `grp`. A program takes and returns all parts, laid end to end along the dimension named above; each array names one. Nothing has to cross between parts.
Inputs may be any that keep to these rules, and one draw needn't show every extreme that they name: `picks`: each row of 3 holds distinct block numbers in ascending order; the last is the block that holds position lengths[b] - 1, the others lie before it. Position lengths[b] - 1 is never the first position of its block.
All inputs are finite; a program needn't handle non-finite values.
Results may differ from a plain program's by a relative error of at most 0.0046.
Values may be sent and summed in bfloat16 or wider, within the bound.
A program may use at most 64 MiB of HBM per device.

v0:
```python
import math
import jax
import jax.numpy as jnp
from jax import lax
from jax.sharding import PartitionSpec as P

BLOCK = 512
NEGATIVE = -1e30


def shards(queries, keys, values, picks, lengths):
    rows = queries.shape[0]
    head_dim = queries.shape[2]
    local_len = keys.shape[1]
    kv_heads = keys.shape[2]
    blocks_here = local_len // BLOCK
    seq_index = lax.axis_index("seq")
    all_queries, all_picks = (
        lax.all_gather(queries, "seq", axis=1, tiled=True),
        lax.all_gather(picks, "seq", axis=1, tiled=True),
    )
    heads = all_queries.shape[1]
    group = heads // kv_heads
    grouped = all_queries.reshape(rows, kv_heads, group, head_dim)
    scores = jnp.einsum("bkgd,btkd->bkgt", grouped, keys, preferred_element_type=jnp.float32) * (
        1.0 / math.sqrt(head_dim)
    )
    scores = scores.reshape(rows, kv_heads, group, blocks_here, BLOCK)
    block_ids = seq_index * blocks_here + jnp.arange(blocks_here, dtype=jnp.int32)
    chosen = jnp.any(all_picks[:, :, :, None] == block_ids[None, None, None, :], axis=2)
    chosen = chosen.reshape(rows, kv_heads, group, blocks_here)
    positions = block_ids[:, None] * BLOCK + jnp.arange(BLOCK, dtype=jnp.int32)[None, :]
    inside = positions[None, :, :] < lengths[:, None, None]
    live = jnp.logical_and(chosen[..., None], inside[:, None, None, :, :])
    masked = jnp.where(live, scores, -jnp.inf)
    any_live = jnp.any(live, axis=-1)
    safe_max = jnp.where(any_live, jnp.max(masked, axis=-1), NEGATIVE)
    weight = jnp.exp(masked - safe_max[..., None])
    block_total = jnp.sum(weight, axis=-1)
    rounded = weight.astype(jnp.bfloat16)
    blocked_values = values.reshape(rows, blocks_here, BLOCK, kv_heads, head_dim)
    block_out = jnp.einsum(
        "bkgnt,bntkd->bkgnd", rounded, blocked_values, preferred_element_type=jnp.float32
    )
    device_max = jnp.max(safe_max, axis=-1)
    coef = jnp.exp(safe_max - device_max[..., None])
    partial_out = jnp.sum(block_out * coef[..., None], axis=3).reshape(rows, heads, head_dim)
    partial_total = jnp.sum(block_total * coef, axis=-1).reshape(rows, heads)
    partial_max = device_max.reshape(rows, heads)
    came_out, came_max, came_total = (
        lax.all_to_all(partial_out[None], "seq", split_axis=2, concat_axis=0, tiled=True),
        lax.all_to_all(partial_max[None], "seq", split_axis=2, concat_axis=0, tiled=True),
        lax.all_to_all(partial_total[None], "seq", split_axis=2, concat_axis=0, tiled=True),
    )
    top = jnp.max(came_max, axis=0)
    rescale = jnp.exp(came_max - top[None])
    mine_out = jnp.sum(came_out * rescale[..., None], axis=0)
    mine_total = jnp.sum(came_total * rescale, axis=0)
    return (mine_out / mine_total[..., None]).astype(jnp.bfloat16)


def solution(mesh):
    return jax.shard_map(
        shards,
        mesh=mesh,
        in_specs=(
            P(("grp", "kv"), "seq", None),
            P(("grp", "kv"), "seq", None, None),
            P(("grp", "kv"), "seq", None, None),
            P(("grp", "kv"), "seq", None),
            P(("grp", "kv")),
        ),
        out_specs=P(("grp", "kv"), "seq", None),
        check_vma=False,
    )
```

profile of v0, /device:TPU:0, one launch (start us, length us, event | category | flops | bytes accessed | tf_op | source)
XLA Modules:
  0.0 97.5 jit_solution(2691425866918644044)
XLA Ops:
  0.7 0.8 copy.28
  1.4 28.1 %all_gather.7 = bf16[1,64,128]{2,1,0:T(8,128)(2,1)S(1)} all-gather(bf16[1,8,128]{2,1,0:T(8,128)(2,1)} %param.5), channel_id=1, replica_groups=mesh['grp'=2,'seq'=8,'kv'=2] {'seq'}, dimensions={1}, use_global_device_ids=true | all-gather | bytes 18432 | tf_op jit(solution)/shard_map/all_gather | solution.py:19
  29.5 30.6 %all_gather.6 = s32[1,64,3]{2,0,1:T(1,128)S(1)} all-gather(s32[1,8,3]{2,0,1:T(1,128)S(1)} %copy.28), channel_id=1, replica_groups=mesh['grp'=2,'seq'=8,'kv'=2] {'seq'}, dimensions={1}, use_global_device_ids=true | all-gather | bytes 864 | tf_op jit(solution)/shard_map/all_gather | solution.py:20
  60.1 0.1 compare_reduce_fusion
  60.2 0.1 and.40
  60.4 0.7 and_reduce_fusion
  61.1 3.4 %fusion.4 = f32[8,8,2048]{2,1,0:T(8,128)S(1)} fusion(bf16[2048,8,128]{2,1,0:T(8,128)(2,1)} %bitcast.31, bf16[1,64,128]{2,1,0:T(8,128)(2,1)S(1)} %all_gather.7), kind=kOutput, calls=%fused_computation.4 | convolution fusion | flops 33685504 | bytes 4734976 | tf_op jit(solution)/shard_map/bkgd,btkd->bkgt/dot_general | solution.py:25
  64.5 0.2 fusion.16
  64.8 0.7 broadcast_in_dim_reshape.13
  65.5 3.9 %all-to-all-start.1 = ((f32[1,1,64]{1,0,2:T(1,128)}), f32[1,1,64]{1,0,2:T(1,128)S(1)}, u32[]{:S(2)}, u32[]{:S(2)}) async-start(f32[1,1,64]{1,0,2:T(1,128)} %broadcast_in_dim_reshape.13), calls=%async_computation.1 | async-start | bytes 65536 | tf_op jit(solution)/shard_map/all_to_all | solution.py:52
  69.4 0.3 exponential_reduce_fusion
  69.7 0.7 broadcast_in_dim_reshape.14
  70.4 5.6 %all-to-all-done.1 = f32[1,1,64]{1,0,2:T(1,128)S(1)} async-done(((f32[1,1,64]{1,0,2:T(1,128)}), f32[1,1,64]{1,0,2:T(1,128)S(1)}, u32[]{:S(2)}, u32[]{:S(2)}) %all-to-all-start.1) | async-done | bytes 288 | tf_op jit(solution)/shard_map/all_to_all | solution.py:52
  76.1 3.3 %all-to-all-start.2 = ((f32[1,1,64]{1,0,2:T(1,128)}), f32[1,1,64]{1,0,2:T(1,128)S(1)}, u32[]{:S(2)}, u32[]{:S(2)}) async-start(f32[1,1,64]{1,0,2:T(1,128)} %broadcast_in_dim_reshape.14), calls=%async_computation.2 | async-start | bytes 65536 | tf_op jit(solution)/shard_map/all_to_all | solution.py:53
  79.4 4.1 %fusion.13 = f32[8,8,128]{2,1,0:T(8,128)} fusion(bf16[4,512,8,128]{3,2,1,0:T(8,128)(2,1)} %bitcast.34, f32[8,8,4,512]{3,1,2,0:T(8,128)S(1)} %bitcast.30, f32[8,8,4]{1,2,0:T(4,128)S(1)} %get-tuple-element.8, pred[4,512]{1,0:T(4,128)(4,1)S(1)} %add_compare_fusion, pred[8,8,4]{1,2,0:T(4,128)(4,1)S(1)} %copy.30, f32[8,8,4]{1,2,0:T(4,128)S(1)} %get-tuple-element.6), kind=kOutput, calls=%fused_computation.7 | convolution fusion | flops 34136064 | bytes 4755712 | tf_op jit(solution)/shard_map/bkgnt,bntkd->bkgnd/dot_general | solution.py:42
  83.5 0.6 reduce.12
  84.0 0.1 all_to_all.32
  84.1 0.1 all_to_all.35
  84.2 1.9 %all-to-all-done.2 = f32[1,1,64]{1,0,2:T(1,128)S(1)} async-done(((f32[1,1,64]{1,0,2:T(1,128)}), f32[1,1,64]{1,0,2:T(1,128)S(1)}, u32[]{:S(2)}, u32[]{:S(2)}) %all-to-all-start.2) | async-done | bytes 288 | tf_op jit(solution)/shard_map/all_to_all | solution.py:53
  86.0 4.1 %all-to-all-start = ((f32[1,1,64,128]{3,1,0,2:T(1,128)}), f32[1,1,64,128]{3,1,0,2:T(1,128)S(1)}, u32[]{:S(2)}, u32[]{:S(2)}) async-start(f32[1,1,64,128]{3,1,0,2:T(1,128)} %bitcast.10), calls=%async_computation | async-start | bytes 65536 | tf_op jit(solution)/shard_map/all_to_all | solution.py:51
  90.1 0.6 reduce.13
  90.7 0.1 all_to_all.34
  90.8 6.0 %all-to-all-done = f32[1,1,64,128]{3,1,0,2:T(1,128)S(1)} async-done(((f32[1,1,64,128]{3,1,0,2:T(1,128)}), f32[1,1,64,128]{3,1,0,2:T(1,128)S(1)}, u32[]{:S(2)}, u32[]{:S(2)}) %all-to-all-start) | async-done | bytes 32800 | tf_op jit(solution)/shard_map/all_to_all | solution.py:51
  96.9 0.7 fusion.22
  (11 shorter events, 0.3 us)
Async XLA Ops:
  65.5 10.5 %all-to-all-start.1 = ((f32[1,1,64]{1,0,2:T(1,128)}), f32[1,1,64]{1,0,2:T(1,128)S(1)}, u32[]{:S(2)}, u32[]{:S(2)}) async-start(f32[1,1,64]{1,0,2:T(1,128)} %broadcast_in_dim_reshape.13), calls=%async_computation.1 | async-start | bytes 65536 | tf_op jit(solution)/shard_map/all_to_all | solution.py:52
  76.1 10.0 %all-to-all-start.2 = ((f32[1,1,64]{1,0,2:T(1,128)}), f32[1,1,64]{1,0,2:T(1,128)S(1)}, u32[]{:S(2)}, u32[]{:S(2)}) async-start(f32[1,1,64]{1,0,2:T(1,128)} %broadcast_in_dim_reshape.14), calls=%async_computation.2 | async-start | bytes 65536 | tf_op jit(solution)/shard_map/all_to_all | solution.py:53
  86.0 10.8 %all-to-all-start = ((f32[1,1,64,128]{3,1,0,2:T(1,128)}), f32[1,1,64,128]{3,1,0,2:T(1,128)S(1)}, u32[]{:S(2)}, u32[]{:S(2)}) async-start(f32[1,1,64,128]{3,1,0,2:T(1,128)} %bitcast.10), calls=%async_computation | async-start | bytes 65536 | tf_op jit(solution)/shard_map/all_to_all | solution.py:51
where the time goes:
time: 98 us; the launch traced here: 97.5 us
  blocking collectives  58.7 us (60%)
  waiting for transfers between devices  13.5 us (14%)
  starting transfers between devices  11.3 us (12%)
  matrix products  7.44 us (8%)
  other arithmetic  3.38 us (3%)
  local copies, waits for them, and re-layouts  2.59 us (3%)
    all_gather x1, blocking collectives, shards(): lax.all_gather(picks, 'seq', axis=1, tiled=True)  30.6 us
    all_gather x1, blocking collectives, shards(): lax.all_gather(queries, 'seq', axis=1, tiled=True)  28.1 us
    all_to_all x1, waiting for transfers between devices, shards(): lax.all_to_all(partial_out[None], 'seq', split_axis=2, concat_axis=0, til...  5.99 us
    all_to_all x1, waiting for transfers between devices, shards(): lax.all_to_all(partial_max[None], 'seq', split_axis=2, concat_axis=0, til...  5.64 us
    all_to_all x1, starting transfers between devices, shards(): lax.all_to_all(partial_out[None], 'seq', split_axis=2, concat_axis=0, til...  4.09 us
    dot_general x1, matrix products, shards(): jnp.einsum('bkgnt,bntkd->bkgnd', rounded, blocked_values, preferred_eleme...  4.05 us
    all_to_all x1, starting transfers between devices, shards(): lax.all_to_all(partial_max[None], 'seq', split_axis=2, concat_axis=0, til...  3.86 us
    dot_general x1, matrix products, shards(): jnp.einsum('bkgd,btkd->bkgt', grouped, keys, preferred_element_type=jnp.f...  3.38 us
  transfers between devices with their start and end apart: 3, of which 3 were waited for; matrix products, arithmetic and copies ran while one was open for 6% of the time, Pallas kernels for 0%

commit v1 on v0

--- a/solution.py
+++ b/solution.py
@@ -49,7 +49,12 @@
     partial_max = device_max.reshape(rows, heads)
     came_out, came_max, came_total = (
         lax.all_to_all(partial_out[None], "seq", split_axis=2, concat_axis=0, tiled=True),
-        lax.all_to_all(partial_max[None], "seq", split_axis=2, concat_axis=0, tiled=True),
+        jnp.concatenate(
+            lax.all_to_all(
+                jnp.stack(jnp.split(partial_max[None], lax.axis_size("seq"), axis=2)), "seq", 0, 0
+            ),
+            axis=0,
+        ),
         lax.all_to_all(partial_total[None], "seq", split_axis=2, concat_axis=0, tiled=True),
     )
     top = jnp.max(came_max, axis=0)

time: 98 us -> 99.2 us (1.012)
  local copies, waits for them, and re-layouts: 2.59 us -> 6.65 us
  waiting for transfers between devices: 13.5 us -> 10.2 us
  starting transfers between devices: 11.3 us -> 12.3 us
    unnamed x1 -> x8, local copies, waits for them, and re-layouts: 0.76 us -> 4.95 us
    all_to_all x1, waiting for transfers between devices: 5.64 us -> 1.8 us  [shards(): lax.all_to_all(jnp.stack(jnp.split(partial_max[None], lax.axis_size('seq'...]
  transfers between devices with their start and end apart: 3 -> 3, of which waited for: 3 -> 3; matrix products, arithmetic and copies ran while one was open for 6% -> 10% of each run, Pallas kernels for 0% -> 0%
where the time goes in v1:
time: 99.2 us; the launch traced here: 98.8 us
  blocking collectives  58.7 us (59%)
  starting transfers between devices  12.3 us (12%)
  waiting for transfers between devices  10.2 us (10%)
  matrix products  7.43 us (7%)
  local copies, waits for them, and re-layouts  6.65 us (7%)
  other arithmetic  2.84 us (3%)
    all_gather x1, blocking collectives, shards(): lax.all_gather(picks, 'seq', axis=1, tiled=True)  30.6 us
    all_gather x1, blocking collectives, shards(): lax.all_gather(queries, 'seq', axis=1, tiled=True)  28.1 us
    all_to_all x1, waiting for transfers between devices, shards(): lax.all_to_all(partial_out[None], 'seq', split_axis=2, concat_axis=0, til...  6.63 us
    unnamed x8, local copies, waits for them, and re-layouts  4.95 us
    all_to_all x1, starting transfers between devices, shards(): lax.all_to_all(jnp.stack(jnp.split(partial_max[None], lax.axis_size('seq'...  4.24 us
    all_to_all x1, starting transfers between devices, shards(): lax.all_to_all(partial_out[None], 'seq', split_axis=2, concat_axis=0, til...  4.2 us
    dot_general x1, matrix products, shards(): jnp.einsum('bkgnt,bntkd->bkgnd', rounded, blocked_values, preferred_eleme...  4.05 us
    all_to_all x1, starting transfers between devices, shards(): lax.all_to_all(partial_total[None], 'seq', split_axis=2, concat_axis=0, t...  3.86 us
  transfers between devices with their start and end apart: 3, of which 3 were waited for; matrix products, arithmetic and copies ran while one was open for 10% of the time, Pallas kernels for 0%

profile of v1, /device:TPU:0, one launch (start us, length us, event | category | flops | bytes accessed | tf_op | source)
XLA Modules:
  0.0 98.8 jit_solution(16684929771123456427)
XLA Ops:
  0.0 28.1 %all_gather.7 = bf16[1,64,128]{2,1,0:T(8,128)(2,1)S(1)} all-gather(bf16[1,8,128]{2,1,0:T(8,128)(2,1)} %param.5), channel_id=1, replica_groups=mesh['grp'=2,'seq'=8,'kv'=2] {'seq'}, dimensions={1}, use_global_device_ids=true | all-gather | bytes 18432 | tf_op jit(solution)/shard_map/all_gather | solution.py:19
  28.7 0.8 copy.26
  29.5 30.6 %all_gather.6 = s32[1,64,3]{2,0,1:T(1,128)S(1)} all-gather(s32[1,8,3]{2,0,1:T(1,128)S(1)} %copy.26), channel_id=1, replica_groups=mesh['grp'=2,'seq'=8,'kv'=2] {'seq'}, dimensions={1}, use_global_device_ids=true | all-gather | bytes 864 | tf_op jit(solution)/shard_map/all_gather | solution.py:20
  60.4 3.4 %fusion.4 = f32[8,8,2048]{2,1,0:T(8,128)S(1)} fusion(bf16[2048,8,128]{2,1,0:T(8,128)(2,1)} %bitcast.49, bf16[1,64,128]{2,1,0:T(8,128)(2,1)S(1)} %all_gather.7), kind=kOutput, calls=%fused_computation.4 | convolution fusion | flops 33685504 | bytes 4734976 | tf_op jit(solution)/shard_map/bkgd,btkd->bkgt/dot_general | solution.py:25
  63.8 0.7 and_reduce_fusion
  64.8 0.3 exponential_reduce_fusion
  65.2 0.7 broadcast_in_dim_reshape.13
  65.9 3.9 %all-to-all-start.2 = ((f32[1,1,64]{1,0,2:T(1,128)}), f32[1,1,64]{1,0,2:T(1,128)S(1)}, u32[]{:S(2)}, u32[]{:S(2)}) async-start(f32[1,1,64]{1,0,2:T(1,128)} %broadcast_in_dim_reshape.13), calls=%async_computation.2 | async-start | bytes 65536 | tf_op jit(solution)/shard_map/all_to_all | solution.py:58
  69.8 0.5 constant_dynamic-update-slice_fusion.7
  70.3 0.6 constant_dynamic-update-slice_fusion.6
  71.0 0.6 constant_dynamic-update-slice_fusion.5
  71.6 0.6 constant_dynamic-update-slice_fusion.4
  72.2 0.6 constant_dynamic-update-slice_fusion.3
  72.8 0.6 constant_dynamic-update-slice_fusion.2
  73.4 0.6 constant_dynamic-update-slice_fusion.1
  74.0 0.7 constant_dynamic-update-slice_fusion
  74.7 1.8 %all-to-all-done.2 = f32[1,1,64]{1,0,2:T(1,128)S(1)} async-done(((f32[1,1,64]{1,0,2:T(1,128)}), f32[1,1,64]{1,0,2:T(1,128)S(1)}, u32[]{:S(2)}, u32[]{:S(2)}) %all-to-all-start.2) | async-done | bytes 288 | tf_op jit(solution)/shard_map/all_to_all | solution.py:58
  76.4 4.2 %all-to-all-start.1 = ((f32[8,1,1,8]{3,2,1,0:T(1,128)}), f32[8,1,1,8]{3,2,1,0:T(1,128)S(1)}, u32[]{:S(2)}, u32[]{:S(2)}) async-start(f32[8,1,1,8]{3,2,1,0:T(1,128)} %constant_dynamic-update-slice_fusion), calls=%async_computation.1 | async-start | bytes 8192 | tf_op jit(solution)/shard_map/all_to_all | solution.py:53
  80.7 4.0 %fusion.13 = f32[8,8,128]{2,1,0:T(8,128)} fusion(bf16[4,512,8,128]{3,2,1,0:T(8,128)(2,1)} %bitcast.54, f32[8,8,4,512]{3,1,2,0:T(8,128)S(1)} %bitcast.48, f32[8,8,4]{1,2,0:T(4,128)S(1)} %get-tuple-element.8, pred[4,512]{1,0:T(4,128)(4,1)S(1)} %add_compare_fusion, pred[8,8,4]{1,2,0:T(4,128)(4,1)S(1)} %copy.28, f32[8,8,4]{1,2,0:T(4,128)S(1)} %get-tuple-element.6), kind=kOutput, calls=%fused_computation.7 | convolution fusion | flops 34136064 | bytes 4755712 | tf_op jit(solution)/shard_map/bkgnt,bntkd->bkgnd/dot_general | solution.py:42
  84.7 0.6 reduce.13
  85.3 1.8 %all-to-all-done.1 = f32[8,1,1,8]{3,2,1,0:T(1,128)S(1)} async-done(((f32[8,1,1,8]{3,2,1,0:T(1,128)}), f32[8,1,1,8]{3,2,1,0:T(1,128)S(1)}, u32[]{:S(2)}, u32[]{:S(2)}) %all-to-all-start.1) | async-done | bytes 288 | tf_op jit(solution)/shard_map/all_to_all | solution.py:53
  87.1 4.2 %all-to-all-start = ((f32[1,1,64,128]{3,1,0,2:T(1,128)}), f32[1,1,64,128]{3,1,0,2:T(1,128)S(1)}, u32[]{:S(2)}, u32[]{:S(2)}) async-start(f32[1,1,64,128]{3,1,0,2:T(1,128)} %bitcast.10), calls=%async_computation | async-start | bytes 65536 | tf_op jit(solution)/shard_map/all_to_all | solution.py:51
  91.4 6.6 %all-to-all-done = f32[1,1,64,128]{3,1,0,2:T(1,128)S(1)} async-done(((f32[1,1,64,128]{3,1,0,2:T(1,128)}), f32[1,1,64,128]{3,1,0,2:T(1,128)S(1)}, u32[]{:S(2)}, u32[]{:S(2)}) %all-to-all-start) | async-done | bytes 32800 | tf_op jit(solution)/shard_map/all_to_all | solution.py:51
  98.1 0.7 fusion.22
  (16 shorter events, 0.9 us)
Async XLA Ops:
  65.9 10.5 %all-to-all-start.2 = ((f32[1,1,64]{1,0,2:T(1,128)}), f32[1,1,64]{1,0,2:T(1,128)S(1)}, u32[]{:S(2)}, u32[]{:S(2)}) async-start(f32[1,1,64]{1,0,2:T(1,128)} %broadcast_in_dim_reshape.13), calls=%async_computation.2 | async-start | bytes 65536 | tf_op jit(solution)/shard_map/all_to_all | solution.py:58
  76.4 10.7 %all-to-all-start.1 = ((f32[8,1,1,8]{3,2,1,0:T(1,128)}), f32[8,1,1,8]{3,2,1,0:T(1,128)S(1)}, u32[]{:S(2)}, u32[]{:S(2)}) async-start(f32[8,1,1,8]{3,2,1,0:T(1,128)} %constant_dynamic-update-slice_fusion), calls=%async_computation.1 | async-start | bytes 8192 | tf_op jit(solution)/shard_map/all_to_all | solution.py:53
  87.1 10.9 %all-to-all-start = ((f32[1,1,64,128]{3,1,0,2:T(1,128)}), f32[1,1,64,128]{3,1,0,2:T(1,128)S(1)}, u32[]{:S(2)}, u32[]{:S(2)}) async-start(f32[1,1,64,128]{3,1,0,2:T(1,128)} %bitcast.10), calls=%async_computation | async-start | bytes 65536 | tf_op jit(solution)/shard_map/all_to_all | solution.py:51
